TPU v7x, 32 devices: a whole 2x2x4 slice. The times are simulated.
32 devices in a mesh: gx: 4 (over y, x), gy: 8 (over z, core).
Axes of the slice: x: 2, y: 2, z: 4, core: 2. Of those that a mesh axis runs over, the one named last changes fastest.
Arguments:
- species_means: bfloat16 [8, 16, 120, 512], P(None, 'gy', None, 'gx'), may hold values from 0.19921875 to 5
- zonal_edge_velocity: float32 [16, 120, 512], P('gy', None, 'gx'), may hold values from -6 to 6
- meridional_edge_velocity: float32 [16, 120, 512], P('gy', None, 'gx'), may hold values from -6 to 6
- scaled_warmth: float32 [16, 120, 512], P('gy', None, 'gx'), may hold values from 0.5 to 2
- donor_depths: float32 [16, 120, 512], P('gy', None, 'gx'), may hold values from 0.5 to 2
- leading_donor_level: int32 [16, 120, 512], P('gy', None, 'gx'), may hold values from 0 to 118, as said below
- opening_share: bfloat16 [16, 120, 512], P('gy', None, 'gx'), may hold values from 0 to 0.44921875
- closing_share: bfloat16 [16, 120, 512], P('gy', None, 'gx'), may hold values from 0.546875 to 1
Outputs:
- tracers_out: float32 [8, 16, 120, 512], P(None, 'gy', None, 'gx')
- regridded_zonal: float32 [16, 120, 512], P('gy', None, 'gx')
- regridded_meridional: float32 [16, 120, 512], P('gy', None, 'gx')
- adjusted_warmth: float32 [16, 120, 512], P('gy', None, 'gx')
Inputs may be any that keep to these rules, and one draw needn't show every extreme that they name: Target layer k draws on source layers leading_donor_level and leading_donor_level + 1, and leading_donor_level lies within 2 of k.
All inputs are finite; a program needn't handle non-finite values.
Results may differ from a plain program's by a relative error of at most 0.0003.
Values sent between devices are 32-bit elements; how exact they have to be, the bound alone decides.
A program may use at most 64 MiB of HBM per device.

v0:
```python
import jax
import jax.numpy as jnp
from jax import lax
from jax.sharding import PartitionSpec as P

thermal_rescale_factor = 3.5
offsets_all = (-2, -1, 0, 1, 2, 3)


def passed_along(value, axis, steps):
    count = lax.axis_size(axis)
    pairs = [(source, (source + steps) % count) for source in range(count)]
    return lax.ppermute(value, axis, pairs)


def ppm_parts(values):
    layers = values.shape[-2]
    top_edge = 1.5 * values[..., 0:1, :] - 0.5 * values[..., 1:2, :]
    second_edge = 0.5 * (values[..., 0:1, :] + values[..., 1:2, :])
    inner_edge = 7.0 / 12.0 * (
        values[..., 1 : layers - 2, :] + values[..., 2 : layers - 1, :]
    ) - 1.0 / 12.0 * (values[..., 0 : layers - 3, :] + values[..., 3:layers, :])
    lower_edge = 0.5 * (
        values[..., layers - 2 : layers - 1, :] + values[..., layers - 1 : layers, :]
    )
    bottom_edge = (
        1.5 * values[..., layers - 1 : layers, :] - 0.5 * values[..., layers - 2 : layers - 1, :]
    )
    edge_values = jnp.concatenate(
        [top_edge, second_edge, inner_edge, lower_edge, bottom_edge], axis=-2
    )
    left_edge = edge_values[..., :layers, :]
    right_edge = edge_values[..., 1:, :]
    return (left_edge, right_edge - left_edge, 6.0 * values - 3.0 * (left_edge + right_edge))


def shifted_layers(values, amount):
    layers = values.shape[-2]
    if amount == 0:
        return values
    if amount > 0:
        filler = jnp.zeros(values.shape[:-2] + (amount, values.shape[-1]), values.dtype)
        return jnp.concatenate([values[..., amount:, :], filler], axis=-2)
    filler = jnp.zeros(values.shape[:-2] + (-amount, values.shape[-1]), values.dtype)
    return jnp.concatenate([filler, values[..., : layers + amount, :]], axis=-2)


def pick_layers(values, masks):
    total = jnp.zeros(values.shape, jnp.float32)
    for amount, selector in zip(offsets_all, masks):
        total = total + jnp.where(selector, shifted_layers(values, amount), 0.0)
    return total


def build_operator(donor_depths, leading_donor_level, opening_share, closing_share):
    start_frac = opening_share.astype(jnp.float32)
    end_frac = closing_share.astype(jnp.float32)
    layer_offset = leading_donor_level - lax.broadcasted_iota(
        jnp.int32, leading_donor_level.shape, 1
    )
    first_masks = [layer_offset == amount for amount in offsets_all]
    second_masks = [layer_offset + 1 == amount for amount in offsets_all]
    weight_first = (1.0 - start_frac) * pick_layers(donor_depths, first_masks)
    weight_second = end_frac * pick_layers(donor_depths, second_masks)
    linear_first = 0.5 * (start_frac + 1.0)
    square_first = linear_first - (start_frac * start_frac + start_frac + 1.0) / 3.0
    linear_second = 0.5 * end_frac
    square_second = linear_second - end_frac * end_frac / 3.0
    return (
        first_masks,
        second_masks,
        weight_first,
        weight_second,
        linear_first,
        square_first,
        linear_second,
        square_second,
    )


def multiply_by_regrid_operator(operator, values):
    (
        first_masks,
        second_masks,
        weight_first,
        weight_second,
        linear_first,
        square_first,
        linear_second,
        square_second,
    ) = operator
    left_edge, edge_slope, curvature = ppm_parts(values)
    mean_first = (
        pick_layers(left_edge, first_masks)
        + pick_layers(edge_slope, first_masks) * linear_first
        + pick_layers(curvature, first_masks) * square_first
    )
    mean_second = (
        pick_layers(left_edge, second_masks)
        + pick_layers(edge_slope, second_masks) * linear_second
        + pick_layers(curvature, second_masks) * square_second
    )
    return (weight_first * mean_first + weight_second * mean_second) / (
        weight_first + weight_second
    )


def local(
    species_means,
    zonal_edge_velocity,
    meridional_edge_velocity,
    scaled_warmth,
    donor_depths,
    leading_donor_level,
    opening_share,
    closing_share,
):
    vertical_regrid_operator = build_operator(
        donor_depths, leading_donor_level, opening_share, closing_share
    )
    regridded_depths = vertical_regrid_operator[2] + vertical_regrid_operator[3]
    mass_before = jnp.sum(species_means.astype(jnp.float32) * donor_depths, axis=(1, 2, 3))
    interior_u_faces = 0.5 * jnp.sum(
        0.5
        * (donor_depths[:-1] + donor_depths[1:])
        * zonal_edge_velocity[:-1]
        * zonal_edge_velocity[:-1]
    )
    interior_v_faces = 0.5 * jnp.sum(
        0.5
        * (donor_depths[:, :, :-1] + donor_depths[:, :, 1:])
        * meridional_edge_velocity[:, :, :-1]
        * meridional_edge_velocity[:, :, :-1]
    )
    local_prior_totals = (
        thermal_rescale_factor * jnp.sum(donor_depths * scaled_warmth)
        + interior_u_faces
        + interior_v_faces
    )
    from_south = passed_along(zonal_edge_velocity[-1:], "gy", 1)
    u_paired = multiply_by_regrid_operator(
        vertical_regrid_operator,
        jnp.stack(
            [zonal_edge_velocity, jnp.concatenate([from_south, zonal_edge_velocity[:-1]], axis=0)]
        ),
    )
    u_cross = u_paired[1]
    returned = passed_along(
        jnp.stack([u_cross[0:1], donor_depths[0:1], regridded_depths[0:1]]), "gy", -1
    )
    north_thick = returned[2]
    edge_u = 0.5 * jnp.sum(
        0.5
        * (donor_depths[-1:] + returned[1])
        * zonal_edge_velocity[-1:]
        * zonal_edge_velocity[-1:]
    )
    regridded_zonal = 0.5 * (u_paired[0] + jnp.concatenate([u_cross[1:], returned[0]], axis=0))
    zonal_following = 0.5 * jnp.sum(
        0.5
        * (regridded_depths + jnp.concatenate([regridded_depths[1:], north_thick], axis=0))
        * regridded_zonal
        * regridded_zonal
    )
    from_west = passed_along(meridional_edge_velocity[:, :, -1:], "gx", 1)
    v_paired = multiply_by_regrid_operator(
        vertical_regrid_operator,
        jnp.stack(
            [
                meridional_edge_velocity,
                jnp.concatenate([from_west, meridional_edge_velocity[:, :, :-1]], axis=2),
            ]
        ),
    )
    v_cross = v_paired[1]
    v_returned = passed_along(
        jnp.stack([v_cross[:, :, 0:1], donor_depths[:, :, 0:1], regridded_depths[:, :, 0:1]]),
        "gx",
        -1,
    )
    regridded_meridional = 0.5 * (
        v_paired[0] + jnp.concatenate([v_cross[:, :, 1:], v_returned[0]], axis=2)
    )
    edge_v = 0.5 * jnp.sum(
        0.5
        * (donor_depths[:, :, -1:] + v_returned[1])
        * meridional_edge_velocity[:, :, -1:]
        * meridional_edge_velocity[:, :, -1:]
    )
    meridional_following = 0.5 * jnp.sum(
        0.5
        * (regridded_depths + jnp.concatenate([regridded_depths[:, :, 1:], v_returned[2]], axis=2))
        * regridded_meridional
        * regridded_meridional
    )
    tracer_new = multiply_by_regrid_operator(
        vertical_regrid_operator, species_means.astype(jnp.float32)
    )
    regridded_warmth = multiply_by_regrid_operator(vertical_regrid_operator, scaled_warmth)
    mass_after = jnp.sum(tracer_new * regridded_depths, axis=(1, 2, 3))
    aggregate_regridded = jnp.sum(regridded_depths)
    kinetic_thermal_following = (
        thermal_rescale_factor * jnp.sum(regridded_depths * regridded_warmth)
        + zonal_following
        + meridional_following
    )
    mass_total_before, mass_total_after, scalars = lax.psum(
        (
            mass_before,
            mass_after,
            jnp.stack(
                [
                    local_prior_totals + edge_u + edge_v,
                    kinetic_thermal_following,
                    aggregate_regridded,
                ]
            ),
        ),
        ("gx", "gy"),
    )
    enthalpy_global_preceding = scalars[0]
    enthalpy_global_following = scalars[1]
    thick_total = scalars[2]
    tracers_out = (
        tracer_new + ((mass_total_before - mass_total_after) / thick_total)[:, None, None, None]
    )
    adjusted_warmth = regridded_warmth + (enthalpy_global_preceding - enthalpy_global_following) / (
        thermal_rescale_factor * thick_total
    )
    return (tracers_out, regridded_zonal, regridded_meridional, adjusted_warmth)


def solution(mesh):
    in_specs = (
        P(None, "gy", None, "gx"),
        P("gy", None, "gx"),
        P("gy", None, "gx"),
        P("gy", None, "gx"),
        P("gy", None, "gx"),
        P("gy", None, "gx"),
        P("gy", None, "gx"),
        P("gy", None, "gx"),
    )
    out_specs = (
        P(None, "gy", None, "gx"),
        P("gy", None, "gx"),
        P("gy", None, "gx"),
        P("gy", None, "gx"),
    )
    return jax.shard_map(local, mesh=mesh, in_specs=in_specs, out_specs=out_specs, check_vma=False)
```

profile of v0, /device:TPU:0, one launch (start us, length us, event | category | flops | bytes accessed | tf_op | source)
XLA Modules:
  0.0 95.7 jit_solution(4133730569461327342)
XLA Ops:
  0.6 1.7 %slice.551 = f32[2,120,1]{2,1,0:T(8,128)} slice(f32[2,120,128]{2,1,0:T(8,128)} %param.10), slice={[0:2], [0:120], [127:128]} | slice | bytes 1920 | tf_op jit(solution)/shard_map/slice | solution.py:165
  2.3 3.0 %collective-permute-start.2 = (f32[2,120,1]{2,1,0:T(8,128)}, f32[2,120,1]{2,1,0:T(8,128)S(1)}, u32[]{:S(2)}, u32[]{:S(2)}) collective-permute-start(f32[2,120,1]{2,1,0:T(8,128)} %slice.551), channel_id=1, source_target_pairs={{0,8},{8,16},{16,24},{24,0},{1,9},{9,17},{17,25},{25,1},{2,10},{10... | collective-permute-start | bytes 2888 | tf_op jit(solution)/shard_map/ppermute | solution.py:13
  5.3 0.6 fusion.103
  6.0 0.0 copy-start.2
  6.0 1.0 %copy-done.2 = bf16[8,2,120,128]{3,2,1,0:T(8,128)(2,1)S(1)} copy-done((bf16[8,2,120,128]{3,2,1,0:T(8,128)(2,1)S(1)}, bf16[8,2,120,128]{3,2,1,0:T(8,128)(2,1)}, u32[]{:S(2)}) %copy-start.2) | copy-done | bytes 491544
  7.0 0.1 convert_element_type.11
  7.1 0.4 fusion.5
  7.5 0.6 fusion.7
  8.0 0.1 slice.631
  8.1 0.4 fusion.86
  8.5 0.4 fusion.87
  8.9 0.1 slice.626
  8.9 0.1 fusion
  9.0 0.1 pad_maximum_fusion.2
  9.1 0.1 pad_maximum_fusion.3
  9.2 0.8 copy-done.1
  10.0 0.8 fusion.46
  10.8 0.1 copy-done.12
  10.8 0.0 copy-done.13
  10.9 0.1 copy-done.15
  11.0 0.4 fusion.51
  11.4 0.1 slice_reduce_fusion
  11.5 0.7 fusion.102
  12.2 0.3 copy-done.3
  12.6 0.7 fusion.61
  13.3 0.8 fusion.98
  14.1 0.8 fusion.99
  14.9 0.7 fusion.40
  15.5 0.7 pad_maximum_fusion.20
  16.2 7.7 %multiply_reduce_fusion = (f32[8]{0:T(128)S(1)}, f32[8,2,120,128]{3,2,1,0:T(8,128)S(1)}) fusion(f32[2,120,128]{2,1,0:T(8,128)S(1)} %get-tuple-element.125, f32[2,120,128]{2,1,0:T(8,128)S(1)} %get-tuple-element.141, f32[2,120,128]{2,1,0:T(8,128)S(1)} %get-tuple-element.140, pred[2,120,128]{2,1,0:T(8,128)(4,1)S(1)} %get-tuple-element.127, ...), kind=kLoop, calls=%fused_computation.18 | loop fusion | flops 24084472 | bytes 17244192 | tf_op jit(solution)/shard_map/reduce_sum | solution.py:200
  24.0 0.8 slice.715
  24.7 0.7 slice.709
  25.4 0.7 slice.704
  26.0 0.1 copy.189
  27.4 0.1 maximum_bitcast_fusion.1
  27.5 0.1 fusion.19
  27.6 0.1 fusion.38
  28.1 1.0 %add_divide_fusion.1 = f32[2,2,120,128]{3,2,1,0:T(8,128)S(1)} fusion(f32[2,2,120,128]{3,2,1,0:T(8,128)S(1)} %get-tuple-element.71, f32[2,2,117,128]{3,2,1,0:T(8,128)S(1)} %slice.692, f32[2,2,118,128]{3,2,1,0:T(8,128)S(1)} %get-tuple-element.90, f32[2,2,119,128]{3,2,1,0:T(8,128)S(1)} %get-tuple-element.92, f32[2,2,119,128]{3,2,1,0:T(8,128)S(1)} %get-tuple-element.91, ...), kind=kLoop, calls=%fused_computation.105 | loop fusion | flops 5591040 | bytes 5355520 | tf_op jit(solution)/shard_map/div | solution.py:103
  29.1 0.1 slice_reduce_fusion.1
  29.2 0.7 slice.718
  29.9 1.2 %collective-permute-start.3 = (f32[3,2,120,1]{2,1,3,0:T(2,128)S(1)}, f32[3,2,120,1]{2,1,3,0:T(2,128)S(1)}, u32[]{:S(2)}, u32[]{:S(2)}) collective-permute-start(f32[3,2,120,1]{2,1,3,0:T(2,128)S(1)} %pad_maximum_fusion.23), channel_id=1, source_target_pairs={{0,24},{8,0},{16,8},{24,16},{1,25},{9,1},{17,9},{25,17},{2,26},{10... | collective-permute-start | bytes 8648 | tf_op jit(solution)/shard_map/ppermute | solution.py:13
  31.1 0.8 maximum_bitcast_fusion
  32.0 0.1 fusion.30
  32.1 0.1 fusion.39
  32.6 1.0 %add_divide_fusion.2 = f32[2,2,120,128]{3,2,1,0:T(8,128)S(1)} fusion(f32[2,2,120,128]{3,2,1,0:T(8,128)S(1)} %get-tuple-element.69, f32[2,2,117,128]{3,2,1,0:T(8,128)S(1)} %slice.660, f32[2,2,118,128]{3,2,1,0:T(8,128)S(1)} %get-tuple-element.79, f32[2,2,119,128]{3,2,1,0:T(8,128)S(1)} %get-tuple-element.81, f32[2,2,119,128]{3,2,1,0:T(8,128)S(1)} %get-tuple-element.80, ...), kind=kLoop, calls=%fused_computation.106 | loop fusion | flops 5591040 | bytes 5355520 | tf_op jit(solution)/shard_map/div | solution.py:103
  33.6 0.6 slice_bitcast_fusion.4
  34.2 0.2 copy-done.11
  34.4 0.7 pad_maximum_fusion.17
  35.1 3.0 %collective-permute-start.1 = (f32[3,1,120,128]{3,2,1,0:T(8,128)}, f32[3,1,120,128]{3,2,1,0:T(8,128)}, u32[]{:S(2)}, u32[]{:S(2)}) collective-permute-start(f32[3,1,120,128]{3,2,1,0:T(8,128)} %pad_maximum_fusion.17), channel_id=1, source_target_pairs={{0,7},{1,0},{2,1},{3,2},{4,3},{5,4},{6,5},{7,6},{8,15},{9,8},{10,9... | collective-permute-start | bytes 552968 | tf_op jit(solution)/shard_map/ppermute | solution.py:13
  38.1 0.8 copy.187
  38.9 0.8 copy.188
  39.7 0.1 copy.180
  39.8 0.8 fusion.47
  41.3 0.0 copy-start.5
  41.3 0.1 collective-permute-done.1
  41.4 0.9 slice_bitcast_fusion.3
  42.4 3.6 %fusion.49 = (f32[]{:T(128)}, f32[]{:T(128)}, f32[]{:T(128)}, f32[]{:T(128)}, f32[2,120,128]{2,1,0:T(8,128)}, /*index=5*/f32[2,120,128]{2,1,0:T(8,128)}, f32[2,120,128]{2,1,0:T(8,128)}) fusion(f32[2,120,128]{2,1,0:T(8,128)S(1)} %get-tuple-element.125, f32[2,120,1]{2,1,0:T(8,128)} %copy.187, f32[2,120,127]{2,1,0:T(8,128)} %slice.715, ...), kind=kLoop, calls=%fused_computation.136 | loop fusion | flops 3839996 | bytes 3906576 | tf_op jit(solution)/shard_map/reduce_sum | solution.py:190
  47.9 1.5 %fusion.63 = (f32[]{:T(128)}, f32[]{:T(128)}) fusion(f32[3,1,120,128]{3,2,1,0:T(8,128)} %collective-permute-done.1, f32[2,120,128]{2,1,0:T(8,128)S(1)} %copy-done, f32[2,120,128]{2,1,0:T(8,128)S(1)} %copy-done.4), kind=kLoop, calls=%fused_computation.176 | loop fusion | flops 153598 | bytes 307208 | tf_op jit(solution)/shard_map/reduce_sum | solution.py:152
  50.7 0.6 pad_maximum_fusion.24
  51.3 39.4 %all-reduce.65 = (f32[8]{0:T(128)S(1)}, f32[8]{0:T(128)S(1)}, f32[3]{0:T(128)S(1)}) all-reduce(f32[8]{0:T(128)S(1)} %get-tuple-element.67, f32[8]{0:T(128)S(1)} %get-tuple-element.36, f32[3]{0:T(128)S(1)} %pad_maximum_fusion.24), channel_id=1, replica_groups=mesh['gx'=4,'gy'=8] {'gx','gy'}, use_global_device_ids=true, to_apply=%region_1.2 | all-reduce | flops 19 | bytes 152 | tf_op jit(solution)/shard_map/psum | solution.py:207
  90.7 0.6 fusion.106
  92.0 0.7 subtract_divide_fusion
  92.7 1.1 %broadcast_add_fusion = f32[8,2,120,128]{3,2,1,0:T(8,128)} fusion(f32[8,2,120,128]{3,2,1,0:T(8,128)S(1)} %get-tuple-element.37, f32[8]{0:T(128)S(1)} %subtract_divide_fusion), kind=kLoop, calls=%fused_computation.57 | loop fusion | flops 245760 | bytes 1966112 | tf_op jit(solution)/shard_map/add | solution.py:225
  95.1 0.7 broadcast_add_fusion.1
  (62 shorter events, 0.8 us)
Async XLA Ops:
  0.6 4.7 %copy-start.4 = (f32[2,120,128]{2,1,0:T(8,128)S(1)}, f32[2,120,128]{2,1,0:T(8,128)}, u32[]{:S(2)}) copy-start(f32[2,120,128]{2,1,0:T(8,128)} %param.9) | copy-start | bytes 368644
  2.3 3.6 %copy-start = (f32[2,120,128]{2,1,0:T(8,128)S(1)}, f32[2,120,128]{2,1,0:T(8,128)}, u32[]{:S(2)}) copy-start(f32[2,120,128]{2,1,0:T(8,128)} %param.12) | copy-start | bytes 368644
  2.3 25.1 %collective-permute-start.2 = (f32[2,120,1]{2,1,0:T(8,128)}, f32[2,120,1]{2,1,0:T(8,128)S(1)}, u32[]{:S(2)}, u32[]{:S(2)}) collective-permute-start(f32[2,120,1]{2,1,0:T(8,128)} %slice.551), channel_id=1, source_target_pairs={{0,8},{8,16},{16,24},{24,0},{1,9},{9,17},{17,25},{25,1},{2,10},{10... | collective-permute-start | bytes 2888 | tf_op jit(solution)/shard_map/ppermute | solution.py:13
  5.9 25.2 %collective-permute-start = (f32[1,120,128]{2,1,0:T(8,128)}, f32[1,120,128]{2,1,0:T(8,128)}, u32[]{:S(2)}, u32[]{:S(2)}) collective-permute-start(f32[1,120,128]{2,1,0:T(8,128)} %get-tuple-element.117), channel_id=1, source_target_pairs={{0,1},{1,2},{2,3},{3,4},{4,5},{5,6},{6,7},{7,0},{8,9},{9,10},{10,1... | collective-permute-start | bytes 184328 | tf_op jit(solution)/shard_map/ppermute | solution.py:13
  6.0 1.0 %copy-start.2 = (bf16[8,2,120,128]{3,2,1,0:T(8,128)(2,1)S(1)}, bf16[8,2,120,128]{3,2,1,0:T(8,128)(2,1)}, u32[]{:S(2)}) copy-start(bf16[8,2,120,128]{3,2,1,0:T(8,128)(2,1)} %param.8) | copy-start | bytes 1474564
  9.1 0.9 copy-start.1
  10.0 0.8 copy-start.12
  10.0 0.9 copy-start.13
  10.0 1.0 %copy-start.15 = (s32[2,120,128]{2,1,0:T(8,128)S(1)}, s32[2,120,128]{2,1,0:T(8,128)}, u32[]{:S(2)}) copy-start(s32[2,120,128]{2,1,0:T(8,128)} %param.13) | copy-start | bytes 368644
  11.5 1.0 copy-start.3
  29.9 8.1 %collective-permute-start.3 = (f32[3,2,120,1]{2,1,3,0:T(2,128)S(1)}, f32[3,2,120,1]{2,1,3,0:T(2,128)S(1)}, u32[]{:S(2)}, u32[]{:S(2)}) collective-permute-start(f32[3,2,120,1]{2,1,3,0:T(2,128)S(1)} %pad_maximum_fusion.23), channel_id=1, source_target_pairs={{0,24},{8,0},{16,8},{24,16},{1,25},{9,1},{17,9},{25,17},{2,26},{10... | collective-permute-start | bytes 8648 | tf_op jit(solution)/shard_map/ppermute | solution.py:13
  33.5 0.8 copy-start.11
  35.1 6.4 %collective-permute-start.1 = (f32[3,1,120,128]{3,2,1,0:T(8,128)}, f32[3,1,120,128]{3,2,1,0:T(8,128)}, u32[]{:S(2)}, u32[]{:S(2)}) collective-permute-start(f32[3,1,120,128]{3,2,1,0:T(8,128)} %pad_maximum_fusion.17), channel_id=1, source_target_pairs={{0,7},{1,0},{2,1},{3,2},{4,3},{5,4},{6,5},{7,6},{8,15},{9,8},{10,9... | collective-permute-start | bytes 552968 | tf_op jit(solution)/shard_map/ppermute | solution.py:13
  38.9 3.4 %copy-start.7 = (f32[2,118,128]{2,1,0:T(8,128)S(1)}, f32[2,118,128]{2,1,0:T(8,128)}, u32[]{:S(2)}) copy-start(f32[2,118,128]{2,1,0:T(8,128)} %get-tuple-element.156) | copy-start | bytes 362500
  38.9 3.5 %copy-start.8 = (f32[2,118,128]{2,1,0:T(8,128)S(1)}, f32[2,118,128]{2,1,0:T(8,128)}, u32[]{:S(2)}) copy-start(f32[2,118,128]{2,1,0:T(8,128)} %get-tuple-element.157) | copy-start | bytes 362500
  38.9 3.5 %copy-start.14 = (f32[1,120,128]{2,1,0:T(8,128)S(1)}, f32[1,120,128]{2,1,0:T(8,128)}, u32[]{:S(2)}) copy-start(f32[1,120,128]{2,1,0:T(8,128)} %get-tuple-element.115) | copy-start | bytes 184324
  39.6 2.7 %copy-start.9 = (f32[2,119,128]{2,1,0:T(8,128)S(1)}, f32[2,119,128]{2,1,0:T(8,128)}, u32[]{:S(2)}) copy-start(f32[2,119,128]{2,1,0:T(8,128)} %get-tuple-element.109) | copy-start | bytes 365572
  41.3 1.1 %copy-start.5 = (f32[2,118,128]{2,1,0:T(8,128)S(1)}, f32[2,118,128]{2,1,0:T(8,128)}, u32[]{:S(2)}) copy-start(f32[2,118,128]{2,1,0:T(8,128)} %get-tuple-element.107) | copy-start | bytes 362500
  41.3 1.1 %copy-start.6 = (f32[2,118,128]{2,1,0:T(8,128)S(1)}, f32[2,118,128]{2,1,0:T(8,128)}, u32[]{:S(2)}) copy-start(f32[2,118,128]{2,1,0:T(8,128)} %get-tuple-element.108) | copy-start | bytes 362500
  92.6 2.4 %copy-start.10 = (f32[2,120,128]{2,1,0:T(8,128)S(1)}, f32[2,120,128]{2,1,0:T(8,128)}, u32[]{:S(2)}) copy-start(f32[2,120,128]{2,1,0:T(8,128)} %get-tuple-element.21) | copy-start | bytes 368644
where the time goes:
time: 96.3 us; the launch traced here: 95.7 us
  blocking collectives  39.4 us (41%)
  other arithmetic  25.4 us (26%)
  local copies, waits for them, and re-layouts  15.2 us (16%)
  between operations  8.29 us (9%)
  starting transfers between devices  7.19 us (7%)
    psum x1, blocking collectives, local(): lax.psum((mass_before, mass_after, jnp.stack([local_prior_totals + edge_u...  39.4 us
    reduce_sum x1, other arithmetic, local(): mass_after = jnp.sum(tracer_new * regridded_depths, axis=(1, 2, 3))  7.73 us
    ppermute x4, starting transfers between devices, passed_along(): return lax.ppermute(value, axis, pairs)  7.19 us
    reduce_sum x1, other arithmetic, local(): jnp.sum(0.5 * (regridded_depths + jnp.concatenate([regridded_depths[:, :,...  3.62 us
    slice x14, local copies, waits for them, and re-layouts, shifted_layers(): return jnp.concatenate([filler, values[..., :layers + amount, :]], axis=-2)  2.64 us
    unnamed x33, local copies, waits for them, and re-layouts  2.56 us
    div x2, other arithmetic, multiply_by_regrid_operator(): (weight_first * mean_first + weight_second * mean_second) / (weight_first...  1.98 us
  transfers between devices with their start and end apart: 4, of which 1 were waited for; matrix products, arithmetic and copies ran while one was open for 28% of the time, Pallas kernels for 0%

commit v1 on v0

--- a/solution.py
+++ b/solution.py
@@ -205,18 +205,21 @@
         + meridional_following
     )
     mass_total_before, mass_total_after, scalars = lax.psum(
-        (
-            mass_before,
-            mass_after,
-            jnp.stack(
-                [
-                    local_prior_totals + edge_u + edge_v,
-                    kinetic_thermal_following,
-                    aggregate_regridded,
-                ]
+        lax.psum(
+            (
+                mass_before,
+                mass_after,
+                jnp.stack(
+                    [
+                        local_prior_totals + edge_u + edge_v,
+                        kinetic_thermal_following,
+                        aggregate_regridded,
+                    ]
+                ),
             ),
+            "gx",
         ),
-        ("gx", "gy"),
+        "gy",
     )
     enthalpy_global_preceding = scalars[0]
     enthalpy_global_following = scalars[1]

time: 96.3 us -> 82.4 us (0.86)
  blocking collectives: 39.4 us -> 24.7 us
    psum x1, blocking collectives: 39.4 us -> 9.45 us  [local(): lax.psum((mass_before, mass_after, jnp.stack([local_prior_totals + edge_u...]
    psum x0 -> x1, blocking collectives: none -> 15.3 us  [local(): lax.psum(lax.psum((mass_before, mass_after, jnp.stack([local_prior_totals...]
  transfers between devices with their start and end apart: 4 -> 4, of which waited for: 1 -> 1; matrix products, arithmetic and copies ran while one was open for 28% -> 34% of each run, Pallas kernels for 0% -> 0%
where the time goes in v1:
time: 82.4 us; the launch traced here: 81.8 us
  other arithmetic  26.3 us (32%)
  blocking collectives  24.7 us (30%)
  local copies, waits for them, and re-layouts  15.3 us (19%)
  between operations  8.13 us (10%)
  starting transfers between devices  7.19 us (9%)
    psum x1, blocking collectives, local(): lax.psum(lax.psum((mass_before, mass_after, jnp.stack([local_prior_totals...  15.3 us
    psum x1, blocking collectives, local(): lax.psum((mass_before, mass_after, jnp.stack([local_prior_totals + edge_u...  9.45 us
    reduce_sum x1, other arithmetic, local(): mass_after = jnp.sum(tracer_new * regridded_depths, axis=(1, 2, 3))  7.75 us
    ppermute x4, starting transfers between devices, passed_along(): return lax.ppermute(value, axis, pairs)  7.19 us
    reduce_sum x1, other arithmetic, local(): jnp.sum(0.5 * (regridded_depths + jnp.concatenate([regridded_depths[:, :,...  3.61 us
    slice x14, local copies, waits for them, and re-layouts, shifted_layers(): return jnp.concatenate([filler, values[..., :layers + amount, :]], axis=-2)  2.65 us
    unnamed x33, local copies, waits for them, and re-layouts  2.59 us
    div x2, other arithmetic, multiply_by_regrid_operator(): (weight_first * mean_first + weight_second * mean_second) / (weight_first...  2 us
  transfers between devices with their start and end apart: 4, of which 1 were waited for; matrix products, arithmetic and copies ran while one was open for 34% of the time, Pallas kernels for 0%

profile of v1, /device:TPU:0, one launch (start us, length us, event | category | flops | bytes accessed | tf_op | source)
XLA Modules:
  0.0 81.8 jit_solution(8116940391586543152)
XLA Ops:
  0.6 1.7 %slice.551 = f32[2,120,1]{2,1,0:T(8,128)} slice(f32[2,120,128]{2,1,0:T(8,128)} %param.10), slice={[0:2], [0:120], [127:128]} | slice | bytes 1920 | tf_op jit(solution)/shard_map/slice | solution.py:165
  2.3 3.0 %collective-permute-start.2 = (f32[2,120,1]{2,1,0:T(8,128)}, f32[2,120,1]{2,1,0:T(8,128)}, u32[]{:S(2)}, u32[]{:S(2)}) collective-permute-start(f32[2,120,1]{2,1,0:T(8,128)} %slice.551), channel_id=1, source_target_pairs={{0,8},{8,16},{16,24},{24,0},{1,9},{9,17},{17,25},{25,1},{2,10},{10... | collective-permute-start | bytes 2888 | tf_op jit(solution)/shard_map/ppermute | solution.py:13
  5.3 0.6 fusion.103
  6.0 0.0 copy-start.2
  6.0 1.0 %copy-done.2 = bf16[8,2,120,128]{3,2,1,0:T(8,128)(2,1)S(1)} copy-done((bf16[8,2,120,128]{3,2,1,0:T(8,128)(2,1)S(1)}, bf16[8,2,120,128]{3,2,1,0:T(8,128)(2,1)}, u32[]{:S(2)}) %copy-start.2) | copy-done | bytes 491544
  7.0 0.1 convert_element_type.11
  7.1 0.4 fusion.5
  7.5 0.6 fusion.7
  8.0 0.1 slice.631
  8.1 0.4 fusion.86
  8.5 0.4 fusion.87
  8.8 0.1 slice.626
  8.9 0.1 fusion
  9.0 0.1 pad_maximum_fusion.2
  9.1 0.1 pad_maximum_fusion.3
  9.2 0.8 copy-done.1
  10.0 0.7 fusion.46
  10.7 0.1 copy-done.12
  10.8 0.0 copy-done.13
  10.9 0.1 copy-done.15
  11.0 0.4 fusion.51
  11.4 0.1 slice_reduce_fusion
  11.5 0.7 fusion.102
  12.2 0.3 copy-done.3
  12.6 0.7 fusion.61
  13.2 0.8 fusion.98
  14.0 0.8 fusion.99
  14.8 0.7 fusion.40
  15.5 0.7 pad_maximum_fusion.20
  16.2 7.7 %multiply_reduce_fusion = (f32[8]{0:T(128)S(1)}, f32[8,2,120,128]{3,2,1,0:T(8,128)S(1)}) fusion(f32[2,120,128]{2,1,0:T(8,128)S(1)} %get-tuple-element.128, f32[2,120,128]{2,1,0:T(8,128)S(1)} %get-tuple-element.144, f32[2,120,128]{2,1,0:T(8,128)S(1)} %get-tuple-element.143, pred[2,120,128]{2,1,0:T(8,128)(4,1)S(1)} %get-tuple-element.130, ...), kind=kLoop, calls=%fused_computation.18 | loop fusion | flops 24084472 | bytes 17244192 | tf_op jit(solution)/shard_map/reduce_sum | solution.py:200
  23.9 0.7 slice.715
  24.7 0.7 slice.709
  25.3 0.7 slice.704
  26.0 0.1 copy.189
  27.3 1.0 %maximum_bitcast_fusion.1 = f32[1,2,120,128]{3,2,1,0:T(8,128)S(1)} fusion(f32[2,120,127]{2,1,0:T(8,128)S(1)} %get-tuple-element.109, f32[2,120,1]{2,1,0:T(8,128)} %collective-permute-done.2), kind=kLoop, calls=%fused_computation.153 | loop fusion | flops 30720 | bytes 245760 | tf_op jit(solution)/shard_map/stack | solution.py:168
  28.3 0.1 fusion.19
  28.4 0.1 fusion.38
  28.8 1.0 %add_divide_fusion.1 = f32[2,2,120,128]{3,2,1,0:T(8,128)S(1)} fusion(f32[2,2,120,128]{3,2,1,0:T(8,128)S(1)} %get-tuple-element.74, f32[2,2,117,128]{3,2,1,0:T(8,128)S(1)} %slice.692, f32[2,2,118,128]{3,2,1,0:T(8,128)S(1)} %get-tuple-element.93, f32[2,2,119,128]{3,2,1,0:T(8,128)S(1)} %get-tuple-element.95, f32[2,2,119,128]{3,2,1,0:T(8,128)S(1)} %get-tuple-element.94, ...), kind=kLoop, calls=%fused_computation.105 | loop fusion | flops 5591040 | bytes 5355520 | tf_op jit(solution)/shard_map/div | solution.py:103
  29.9 0.1 slice_reduce_fusion.1
  30.0 0.8 slice.718
  30.7 1.2 %collective-permute-start.3 = (f32[3,2,120,1]{2,1,3,0:T(2,128)S(1)}, f32[3,2,120,1]{2,1,3,0:T(2,128)S(1)}, u32[]{:S(2)}, u32[]{:S(2)}) collective-permute-start(f32[3,2,120,1]{2,1,3,0:T(2,128)S(1)} %pad_maximum_fusion.23), channel_id=1, source_target_pairs={{0,24},{8,0},{16,8},{24,16},{1,25},{9,1},{17,9},{25,17},{2,26},{10... | collective-permute-start | bytes 8648 | tf_op jit(solution)/shard_map/ppermute | solution.py:13
  32.0 0.8 %maximum_bitcast_fusion = f32[1,2,120,128]{3,2,1,0:T(8,128)S(1)} fusion(f32[1,120,128]{2,1,0:T(8,128)S(1)} %get-tuple-element.121, f32[1,120,128]{2,1,0:T(8,128)} %collective-permute-done), kind=kLoop, calls=%fused_computation.152 | loop fusion | flops 30720 | bytes 245760 | tf_op jit(solution)/shard_map/stack | solution.py:143
  32.8 0.1 fusion.30
  33.0 0.1 fusion.39
  33.4 1.0 %add_divide_fusion.2 = f32[2,2,120,128]{3,2,1,0:T(8,128)S(1)} fusion(f32[2,2,120,128]{3,2,1,0:T(8,128)S(1)} %get-tuple-element.72, f32[2,2,117,128]{3,2,1,0:T(8,128)S(1)} %slice.660, f32[2,2,118,128]{3,2,1,0:T(8,128)S(1)} %get-tuple-element.82, f32[2,2,119,128]{3,2,1,0:T(8,128)S(1)} %get-tuple-element.84, f32[2,2,119,128]{3,2,1,0:T(8,128)S(1)} %get-tuple-element.83, ...), kind=kLoop, calls=%fused_computation.106 | loop fusion | flops 5591040 | bytes 5355520 | tf_op jit(solution)/shard_map/div | solution.py:103
  34.4 0.6 slice_bitcast_fusion.4
  35.0 0.2 copy-done.11
  35.2 0.7 pad_maximum_fusion.17
  35.9 3.0 %collective-permute-start.1 = (f32[3,1,120,128]{3,2,1,0:T(8,128)}, f32[3,1,120,128]{3,2,1,0:T(8,128)}, u32[]{:S(2)}, u32[]{:S(2)}) collective-permute-start(f32[3,1,120,128]{3,2,1,0:T(8,128)} %pad_maximum_fusion.17), channel_id=1, source_target_pairs={{0,7},{1,0},{2,1},{3,2},{4,3},{5,4},{6,5},{7,6},{8,15},{9,8},{10,9... | collective-permute-start | bytes 552968 | tf_op jit(solution)/shard_map/ppermute | solution.py:13
  38.9 0.8 copy.187
  39.7 0.8 copy.188
  40.5 0.1 copy.180
  40.6 0.8 fusion.47
  42.1 0.2 collective-permute-done.1
  42.3 0.9 %slice_bitcast_fusion.3 = (f32[1,120,128]{2,1,0:T(8,128)S(1)}, f32[1,120,128]{2,1,0:T(8,128)S(1)}) fusion(f32[3,1,120,128]{3,2,1,0:T(8,128)} %collective-permute-done.1), kind=kLoop, calls=%fused_computation.177 | loop fusion | bytes 245760 | tf_op jit(solution)/shard_map/squeeze | solution.py:158
  43.2 3.6 %fusion.49 = (f32[]{:T(128)}, f32[]{:T(128)}, f32[]{:T(128)}, f32[]{:T(128)}, f32[2,120,128]{2,1,0:T(8,128)}, /*index=5*/f32[2,120,128]{2,1,0:T(8,128)}, f32[2,120,128]{2,1,0:T(8,128)}) fusion(f32[2,120,128]{2,1,0:T(8,128)S(1)} %get-tuple-element.128, f32[2,120,1]{2,1,0:T(8,128)} %copy.187, f32[2,120,127]{2,1,0:T(8,128)} %slice.715, ...), kind=kLoop, calls=%fused_computation.136 | loop fusion | flops 3839996 | bytes 3906576 | tf_op jit(solution)/shard_map/reduce_sum | solution.py:190
  48.6 1.5 %fusion.63 = (f32[]{:T(128)}, f32[]{:T(128)}) fusion(f32[3,1,120,128]{3,2,1,0:T(8,128)} %collective-permute-done.1, f32[2,120,128]{2,1,0:T(8,128)S(1)} %copy-done, f32[2,120,128]{2,1,0:T(8,128)S(1)} %copy-done.4), kind=kLoop, calls=%fused_computation.176 | loop fusion | flops 153598 | bytes 307208 | tf_op jit(solution)/shard_map/reduce_sum | solution.py:152
  51.4 0.7 pad_maximum_fusion.24
  52.1 9.5 %all-reduce.66 = (f32[8]{0:T(128)S(1)}, f32[8]{0:T(128)S(1)}, f32[3]{0:T(128)S(1)}) all-reduce(f32[8]{0:T(128)S(1)} %get-tuple-element.70, f32[8]{0:T(128)S(1)} %get-tuple-element.39, f32[3]{0:T(128)S(1)} %pad_maximum_fusion.24), channel_id=1, replica_groups=mesh['gx'=4,'gy'=8] {'gx'}, use_global_device_ids=true, to_apply=%region_1.2 | all-reduce | flops 19 | bytes 152 | tf_op jit(solution)/shard_map/psum | solution.py:208
  61.5 15.3 %all-reduce.65 = (f32[8]{0:T(128)S(1)}, f32[8]{0:T(128)S(1)}, f32[3]{0:T(128)S(1)}) all-reduce(f32[8]{0:T(128)S(1)} %get-tuple-element.21, f32[8]{0:T(128)S(1)} %get-tuple-element.22, f32[3]{0:T(128)S(1)} %get-tuple-element.23), channel_id=1, replica_groups=mesh['gx'=4,'gy'=8] {'gy'}, use_global_device_ids=true, to_apply=%region_2.3 | all-reduce | flops 19 | bytes 152 | tf_op jit(solution)/shard_map/psum | solution.py:207
  76.8 0.6 fusion.106
  78.0 0.7 subtract_divide_fusion
  78.7 1.1 %broadcast_add_fusion = f32[8,2,120,128]{3,2,1,0:T(8,128)} fusion(f32[8,2,120,128]{3,2,1,0:T(8,128)S(1)} %get-tuple-element.40, f32[8]{0:T(128)S(1)} %subtract_divide_fusion), kind=kLoop, calls=%fused_computation.57 | loop fusion | flops 245760 | bytes 1966112 | tf_op jit(solution)/shard_map/add | solution.py:228
  81.1 0.7 broadcast_add_fusion.1
  (63 shorter events, 0.8 us)
Async XLA Ops:
  0.6 4.7 %copy-start.4 = (f32[2,120,128]{2,1,0:T(8,128)S(1)}, f32[2,120,128]{2,1,0:T(8,128)}, u32[]{:S(2)}) copy-start(f32[2,120,128]{2,1,0:T(8,128)} %param.9) | copy-start | bytes 368644
  2.3 3.6 %copy-start = (f32[2,120,128]{2,1,0:T(8,128)S(1)}, f32[2,120,128]{2,1,0:T(8,128)}, u32[]{:S(2)}) copy-start(f32[2,120,128]{2,1,0:T(8,128)} %param.12) | copy-start | bytes 368644
  2.3 24.9 %collective-permute-start.2 = (f32[2,120,1]{2,1,0:T(8,128)}, f32[2,120,1]{2,1,0:T(8,128)}, u32[]{:S(2)}, u32[]{:S(2)}) collective-permute-start(f32[2,120,1]{2,1,0:T(8,128)} %slice.551), channel_id=1, source_target_pairs={{0,8},{8,16},{16,24},{24,0},{1,9},{9,17},{17,25},{25,1},{2,10},{10... | collective-permute-start | bytes 2888 | tf_op jit(solution)/shard_map/ppermute | solution.py:13
  5.9 26.0 %collective-permute-start = (f32[1,120,128]{2,1,0:T(8,128)}, f32[1,120,128]{2,1,0:T(8,128)}, u32[]{:S(2)}, u32[]{:S(2)}) collective-permute-start(f32[1,120,128]{2,1,0:T(8,128)} %get-tuple-element.120), channel_id=1, source_target_pairs={{0,1},{1,2},{2,3},{3,4},{4,5},{5,6},{6,7},{7,0},{8,9},{9,10},{10,1... | collective-permute-start | bytes 184328 | tf_op jit(solution)/shard_map/ppermute | solution.py:13
  6.0 1.0 %copy-start.2 = (bf16[8,2,120,128]{3,2,1,0:T(8,128)(2,1)S(1)}, bf16[8,2,120,128]{3,2,1,0:T(8,128)(2,1)}, u32[]{:S(2)}) copy-start(bf16[8,2,120,128]{3,2,1,0:T(8,128)(2,1)} %param.8) | copy-start | bytes 1474564
  9.1 0.9 %copy-start.1 = (f32[2,120,128]{2,1,0:T(8,128)S(1)}, f32[2,120,128]{2,1,0:T(8,128)}, u32[]{:S(2)}) copy-start(f32[2,120,128]{2,1,0:T(8,128)} %param.10) | copy-start | bytes 368644
  10.0 0.8 %copy-start.12 = (bf16[2,120,128]{2,1,0:T(8,128)(2,1)S(1)}, bf16[2,120,128]{2,1,0:T(8,128)(2,1)}, u32[]{:S(2)}) copy-start(bf16[2,120,128]{2,1,0:T(8,128)(2,1)} %param.14) | copy-start | bytes 184324
  10.0 0.9 %copy-start.13 = (bf16[2,120,128]{2,1,0:T(8,128)(2,1)S(1)}, bf16[2,120,128]{2,1,0:T(8,128)(2,1)}, u32[]{:S(2)}) copy-start(bf16[2,120,128]{2,1,0:T(8,128)(2,1)} %param.15) | copy-start | bytes 184324
  10.0 1.0 %copy-start.15 = (s32[2,120,128]{2,1,0:T(8,128)S(1)}, s32[2,120,128]{2,1,0:T(8,128)}, u32[]{:S(2)}) copy-start(s32[2,120,128]{2,1,0:T(8,128)} %param.13) | copy-start | bytes 368644
  11.5 1.0 %copy-start.3 = (f32[2,120,128]{2,1,0:T(8,128)S(1)}, f32[2,120,128]{2,1,0:T(8,128)}, u32[]{:S(2)}) copy-start(f32[2,120,128]{2,1,0:T(8,128)} %param.11) | copy-start | bytes 368644
  30.7 8.2 %collective-permute-start.3 = (f32[3,2,120,1]{2,1,3,0:T(2,128)S(1)}, f32[3,2,120,1]{2,1,3,0:T(2,128)S(1)}, u32[]{:S(2)}, u32[]{:S(2)}) collective-permute-start(f32[3,2,120,1]{2,1,3,0:T(2,128)S(1)} %pad_maximum_fusion.23), channel_id=1, source_target_pairs={{0,24},{8,0},{16,8},{24,16},{1,25},{9,1},{17,9},{25,17},{2,26},{10... | collective-permute-start | bytes 8648 | tf_op jit(solution)/shard_map/ppermute | solution.py:13
  34.4 0.8 %copy-start.11 = (f32[1,1,120,128]{3,2,1,0:T(8,128)S(1)}, f32[1,1,120,128]{3,2,1,0:T(8,128)}, u32[]{:S(2)}) copy-start(f32[1,1,120,128]{3,2,1,0:T(8,128)} %get-tuple-element.119) | copy-start | bytes 184324
  35.9 6.4 %collective-permute-start.1 = (f32[3,1,120,128]{3,2,1,0:T(8,128)}, f32[3,1,120,128]{3,2,1,0:T(8,128)}, u32[]{:S(2)}, u32[]{:S(2)}) collective-permute-start(f32[3,1,120,128]{3,2,1,0:T(8,128)} %pad_maximum_fusion.17), channel_id=1, source_target_pairs={{0,7},{1,0},{2,1},{3,2},{4,3},{5,4},{6,5},{7,6},{8,15},{9,8},{10,9... | collective-permute-start | bytes 552968 | tf_op jit(solution)/shard_map/ppermute | solution.py:13
  39.7 3.4 %copy-start.7 = (f32[2,118,128]{2,1,0:T(8,128)S(1)}, f32[2,118,128]{2,1,0:T(8,128)}, u32[]{:S(2)}) copy-start(f32[2,118,128]{2,1,0:T(8,128)} %get-tuple-element.159) | copy-start | bytes 362500
  39.7 3.5 %copy-start.8 = (f32[2,118,128]{2,1,0:T(8,128)S(1)}, f32[2,118,128]{2,1,0:T(8,128)}, u32[]{:S(2)}) copy-start(f32[2,118,128]{2,1,0:T(8,128)} %get-tuple-element.160) | copy-start | bytes 362500
  39.7 3.5 %copy-start.14 = (f32[1,120,128]{2,1,0:T(8,128)S(1)}, f32[1,120,128]{2,1,0:T(8,128)}, u32[]{:S(2)}) copy-start(f32[1,120,128]{2,1,0:T(8,128)} %get-tuple-element.118) | copy-start | bytes 184324
  40.5 2.7 %copy-start.9 = (f32[2,119,128]{2,1,0:T(8,128)S(1)}, f32[2,119,128]{2,1,0:T(8,128)}, u32[]{:S(2)}) copy-start(f32[2,119,128]{2,1,0:T(8,128)} %get-tuple-element.112) | copy-start | bytes 365572
  42.1 1.1 %copy-start.5 = (f32[2,118,128]{2,1,0:T(8,128)S(1)}, f32[2,118,128]{2,1,0:T(8,128)}, u32[]{:S(2)}) copy-start(f32[2,118,128]{2,1,0:T(8,128)} %get-tuple-element.110) | copy-start | bytes 362500
  42.1 1.1 %copy-start.6 = (f32[2,118,128]{2,1,0:T(8,128)S(1)}, f32[2,118,128]{2,1,0:T(8,128)}, u32[]{:S(2)}) copy-start(f32[2,118,128]{2,1,0:T(8,128)} %get-tuple-element.111) | copy-start | bytes 362500
  78.7 2.4 %copy-start.10 = (f32[2,120,128]{2,1,0:T(8,128)S(1)}, f32[2,120,128]{2,1,0:T(8,128)}, u32[]{:S(2)}) copy-start(f32[2,120,128]{2,1,0:T(8,128)} %get-tuple-element.24) | copy-start | bytes 368644
